TPU v7x, 32 devices: a whole 2x2x4 slice. The times are simulated.
32 devices in a mesh: ep: 32 (over z, y, x, core).
Axes of the slice: x: 2, y: 2, z: 4, core: 2. Of those that a mesh axis runs over, the one named last changes fastest.
Arguments:
- hidden: bfloat16 [16384, 1280], P('ep')
- w_router: float32 [1280, 32], replicated
- expert_ids: int32 [16384, 2], P('ep')
- w_one: bfloat16 [32, 1280, 5120], P('ep')
- w_three: bfloat16 [32, 1280, 5120], P('ep')
- w_two: bfloat16 [32, 5120, 1280], P('ep')
Outputs:
- output: bfloat16 [16384, 1280], P('ep')
All inputs are finite; a program needn't handle non-finite values.
Results may differ from a plain program's by a relative error of at most 0.00867312.
Values are sent between devices in bfloat16 or wider.
A program may use at most 1 GiB of HBM per device.

v0:
```python
import jax
import jax.numpy as jnp
from jax import lax
from jax.sharding import PartitionSpec as P


def route_gates(hidden_loc, w_router, ids_loc):
    logits = jnp.dot(hidden_loc.astype(jnp.float32), w_router, preferred_element_type=jnp.float32)
    prob_vals = jax.nn.softmax(logits, axis=-1)
    picked = jnp.take_along_axis(prob_vals, ids_loc, axis=1)
    return picked / jnp.sum(picked, axis=1, keepdims=True)


def expert_ffn(sorted_rows, group_sizes, w_one, w_three, w_two):
    h_one = lax.ragged_dot(sorted_rows, w_one, group_sizes, preferred_element_type=jnp.float32)
    h_three = lax.ragged_dot(sorted_rows, w_three, group_sizes, preferred_element_type=jnp.float32)
    act_rows = (jax.nn.silu(h_one) * h_three).astype(jnp.bfloat16)
    return lax.ragged_dot(act_rows, w_two, group_sizes, preferred_element_type=jnp.float32).astype(jnp.bfloat16)


def solution(mesh):
    dev_count = mesh.shape["ep"]

    def device_body(hidden_loc, w_router, ids_loc, w_one, w_three, w_two):
        tok_count = hidden_loc.shape[0]
        model_dim = hidden_loc.shape[1]
        local_count = w_one.shape[0]
        row_cap = 4 * tok_count // dev_count
        gate_vals = route_gates(hidden_loc, w_router, ids_loc)
        flat_ids = ids_loc.reshape(-1)
        assign_count = flat_ids.shape[0]
        dest_dev = flat_ids // local_count
        dest_onehot = (dest_dev[:, None] == jnp.arange(dev_count)[None, :]).astype(jnp.int32)
        slot_idx = jnp.sum(jnp.cumsum(dest_onehot, axis=0) * dest_onehot, axis=1) - 1
        slot_pos = dest_dev * row_cap + slot_idx
        src_token = jnp.zeros((dev_count * row_cap,), jnp.int32).at[slot_pos].set(jnp.arange(assign_count, dtype=jnp.int32) // 2)
        send_exp = jnp.full((dev_count * row_cap,), local_count, jnp.int32).at[slot_pos].set(flat_ids % local_count)
        send_rows = jnp.take(hidden_loc, src_token, axis=0).reshape(dev_count, row_cap, model_dim)
        recv_rows = lax.all_to_all(send_rows, "ep", 0, 0, tiled=True)
        recv_exp = lax.all_to_all(send_exp.reshape(dev_count, row_cap), "ep", 0, 0, tiled=True)
        row_exp = recv_exp.reshape(-1)
        sort_order = jnp.argsort(row_exp, stable=True)
        group_sizes = jnp.sum((row_exp[:, None] == jnp.arange(local_count)[None, :]).astype(jnp.int32), axis=0)
        sorted_rows = jnp.take(recv_rows.reshape(dev_count * row_cap, model_dim), sort_order, axis=0)
        out_sorted = expert_ffn(sorted_rows, group_sizes, w_one, w_three, w_two)
        out_rows = jnp.take(out_sorted, jnp.argsort(sort_order), axis=0)
        back_rows = lax.all_to_all(out_rows.reshape(dev_count, row_cap, model_dim), "ep", 0, 0, tiled=True)
        picked_rows = jnp.take(back_rows.reshape(dev_count * row_cap, model_dim), slot_pos, axis=0)
        both_out = picked_rows.reshape(tok_count, 2, model_dim).astype(jnp.float32)
        return jnp.sum(gate_vals[:, :, None] * both_out, axis=1).astype(jnp.bfloat16)

    return jax.shard_map(device_body, mesh=mesh, in_specs=(P("ep", None), P(None, None), P("ep", None), P("ep", None, None), P("ep", None, None), P("ep", None, None)), out_specs=P("ep", None), check_vma=False)
```

profile of v0, /device:TPU:5, one launch (start us, length us, event | category | flops | bytes accessed | tf_op | source)
XLA Modules:
  0.0 509.4 jit_solution(11488250535287325202)
XLA Ops:
  2.0 9.0 %reduce-window.6 = s32[32,8,128]{2,1,0:T(8,128)S(1)} reduce-window(s32[32,8,128]{2,1,0:T(8,128)S(1)} %fusion.2, s32[]{:T(128)} %constant.100.clone.1), window={size=1x1x128 pad=0_0x0_0x127_0}, to_apply=%region_3.4 | reduce-window | flops 4161536 | bytes 262148 | tf_op jit(solution)/shard_map/reduce-window
  11.9 4.3 scatter_custom_fusion.1
  16.9 6.4 %all-to-all-start.1 = ((s32[32,1,64]{2,1,0:T(1,128)}), s32[32,1,64]{2,1,0:T(1,128)S(1)}, u32[]{:S(2)}, u32[]{:S(2)}) async-start(s32[32,1,64]{2,1,0:T(1,128)} %all_to_all.13), calls=%async_computation.1 | async-start | bytes 32768 | tf_op jit(solution)/shard_map/all_to_all | solution.py:40
  27.8 9.9 %gather_fusion = bf16[2048,1280]{1,0:T(8,128)(2,1)} fusion(bf16[512,1280]{1,0:T(8,128)(2,1)S(1)} %copy-done, s32[2048]{0:T(1024)S(1)} %fusion.5), kind=kCustom, calls=%fused_computation.2 | custom fusion | bytes 10493952 | tf_op jit(solution)/shard_map/jit(_take)/gather | solution.py:38
  37.6 5.4 %broadcast_select_fusion.2 = bf16[32,64,1280]{2,1,0:T(8,128)(2,1)} fusion(bf16[32,64,1280]{2,1,0:T(8,128)(2,1)} %bitcast.28, pred[32,64]{1,0:T(8,128)(4,1)S(1)} %broadcast_in_dim.54), kind=kLoop, calls=%fused_computation.11 | loop fusion | flops 2621440 | bytes 10487808 | tf_op jit(solution)/shard_map/jit(_take)/select_n | solution.py:38
  43.0 5.9 %all-to-all-start = ((bf16[32,64,1280]{2,1,0:T(8,128)(2,1)}), bf16[32,64,1280]{2,1,0:T(8,128)(2,1)}, u32[]{:S(2)}, u32[]{:S(2)}) async-start(bf16[32,64,1280]{2,1,0:T(8,128)(2,1)} %broadcast_select_fusion.2), calls=%async_computation | async-start | bytes 10485760 | tf_op jit(solution)/shard_map/all_to_all | solution.py:39
  52.1 5.0 sort.34
  57.2 5.0 sort.35
  62.3 103.0 %all-to-all-done = bf16[32,64,1280]{2,1,0:T(8,128)(2,1)} async-done(((bf16[32,64,1280]{2,1,0:T(8,128)(2,1)}), bf16[32,64,1280]{2,1,0:T(8,128)(2,1)}, u32[]{:S(2)}, u32[]{:S(2)}) %all-to-all-start) | async-done | bytes 5242912 | tf_op jit(solution)/shard_map/all_to_all | solution.py:39
  165.3 15.2 %gather_fusion.3 = bf16[2048,1280]{1,0:T(8,128)(2,1)} fusion(bf16[2048,1280]{1,0:T(8,128)(2,1)} %bitcast.8, s32[2048]{0:T(1024)S(1)} %fusion.6), kind=kCustom, calls=%fused_computation.clone | custom fusion | bytes 10493952 | tf_op jit(solution)/shard_map/jit(_take)/gather | solution.py:44
  180.5 5.4 %broadcast_select_fusion.1 = bf16[2048,1280]{1,0:T(8,128)(2,1)} fusion(bf16[2048,1280]{1,0:T(8,128)(2,1)} %gather_fusion.3, pred[2048]{0:T(1024)(128)(4,1)S(1)} %compare_and_fusion.1), kind=kLoop, calls=%fused_computation.10 | loop fusion | flops 2621440 | bytes 10487808 | tf_op jit(solution)/shard_map/jit(_take)/select_n | solution.py:44
  185.9 20.0 %ragged-dot-none.2 = f32[2048,5120]{1,0:T(8,128)} custom-call(s32[1]{0:T(128)} %get-tuple-element.10, s32[2]{0:T(128)} %get-tuple-element.11, s32[8]{0:T(128)} %get-tuple-element.12, s32[8]{0:T(128)} %get-tuple-element.13, s32[1]{0:T(128)} %get-tuple-element.10, bf16[2048,1280]{1,0:T(8,128)(2,1)} %broadcast_select_fusion.1, bf16[1,1280,5120]{2,1,0:T(8,128)(2,1)} %param.11), custom_call_target="tpu_custom_call" | custom-call | flops 26843545600 | bytes 60293124 | tf_op jit(solution)/shard_map/ragged_dot_general/ragged-dot-none
  205.8 20.2 %ragged-dot-none.1 = f32[2048,5120]{1,0:T(8,128)} custom-call(s32[1]{0:T(128)} %get-tuple-element.10, s32[2]{0:T(128)} %get-tuple-element.11, s32[8]{0:T(128)} %get-tuple-element.12, s32[8]{0:T(128)} %get-tuple-element.13, s32[1]{0:T(128)} %get-tuple-element.10, bf16[2048,1280]{1,0:T(8,128)(2,1)} %broadcast_select_fusion.1, bf16[1,1280,5120]{2,1,0:T(8,128)(2,1)} %param.12), custom_call_target="tpu_custom_call" | custom-call | flops 26843545600 | bytes 60293124 | tf_op jit(solution)/shard_map/ragged_dot_general/ragged-dot-none
  226.1 34.1 %multiply_convert_fusion = bf16[2048,5120]{1,0:T(8,128)(2,1)} fusion(f32[2048,5120]{1,0:T(8,128)} %ragged-dot-none.1, f32[2048,5120]{1,0:T(8,128)} %ragged-dot-none.2), kind=kLoop, calls=%fused_computation.7 | loop fusion | flops 62914560 | bytes 104857600 | tf_op jit(solution)/shard_map/convert_element_type | solution.py:17
  260.1 19.3 %ragged-dot-none = f32[2048,1280]{1,0:T(8,128)} custom-call(s32[1]{0:T(128)} %get-tuple-element.10, s32[2]{0:T(128)} %get-tuple-element.11, s32[8]{0:T(128)} %get-tuple-element.12, s32[8]{0:T(128)} %get-tuple-element.13, s32[1]{0:T(128)} %get-tuple-element.10, bf16[2048,5120]{1,0:T(8,128)(2,1)} %multiply_convert_fusion, bf16[1,5120,1280]{2,1,0:T(8,128)(2,1)} %param.13), custom_call_target="tpu_custom_call" | custom-call | flops 26843545600 | bytes 44564484 | tf_op jit(solution)/shard_map/ragged_dot_general/ragged-dot-none
  279.4 6.9 %convert_element_type.28 = bf16[2048,1280]{1,0:T(8,128)(2,1)} convert(f32[2048,1280]{1,0:T(8,128)} %ragged-dot-none) | non-fusion elementwise | flops 2621440 | bytes 15728640 | tf_op jit(solution)/shard_map/convert_element_type | solution.py:18
  286.3 15.2 %gather_fusion.4 = bf16[2048,1280]{1,0:T(8,128)(2,1)} fusion(bf16[2048,1280]{1,0:T(8,128)(2,1)} %convert_element_type.28, s32[2048]{0:T(1024)S(1)} %fusion.7), kind=kCustom, calls=%fused_computation.1.clone | custom fusion | bytes 10493952 | tf_op jit(solution)/shard_map/jit(_take)/gather | solution.py:46
  301.5 5.4 %broadcast_select_fusion = bf16[2048,1280]{1,0:T(8,128)(2,1)} fusion(bf16[2048,1280]{1,0:T(8,128)(2,1)} %gather_fusion.4, pred[2048]{0:T(1024)(128)(4,1)S(1)} %compare_and_fusion), kind=kLoop, calls=%fused_computation.9 | loop fusion | flops 2621440 | bytes 10487808 | tf_op jit(solution)/shard_map/jit(_take)/select_n | solution.py:46
  306.9 57.7 %all-to-all-start.2 = ((bf16[32,64,1280]{2,1,0:T(8,128)(2,1)}), bf16[32,64,1280]{2,1,0:T(8,128)(2,1)}, u32[]{:S(2)}, u32[]{:S(2)}) async-start(bf16[32,64,1280]{2,1,0:T(8,128)(2,1)} %bitcast.29), calls=%async_computation.2 | async-start | bytes 10485760 | tf_op jit(solution)/shard_map/all_to_all | solution.py:47
  365.8 8.6 %gather_fusion.2 = f32[1024]{0:T(1024)S(1)} fusion(f32[512,32]{0,1:T(8,128)S(1)} %fusion.3, s32[1024]{0:T(1024)S(1)} %reshape.171), kind=kCustom, calls=%fused_computation.4 | custom fusion | bytes 16384 | tf_op jit(solution)/shard_map/jit(take_along_axis)/gather | solution.py:10
  375.3 105.6 %all-to-all-done.2 = bf16[32,64,1280]{2,1,0:T(8,128)(2,1)} async-done(((bf16[32,64,1280]{2,1,0:T(8,128)(2,1)}), bf16[32,64,1280]{2,1,0:T(8,128)(2,1)}, u32[]{:S(2)}, u32[]{:S(2)}) %all-to-all-start.2) | async-done | bytes 5242912 | tf_op jit(solution)/shard_map/all_to_all | solution.py:47
  480.9 9.7 %gather_fusion.1 = bf16[1024,1280]{1,0:T(8,128)(2,1)} fusion(bf16[2048,1280]{1,0:T(8,128)(2,1)} %bitcast.10, s32[1024]{0:T(1024)S(1)} %broadcast_clamp_fusion), kind=kCustom, calls=%fused_computation.3 | custom fusion | bytes 5246976 | tf_op jit(solution)/shard_map/jit(_take)/gather | solution.py:48
  490.7 6.5 %gather.23 = bf16[512,2,1280]{2,1,0:T(2,128)(2,1)} reshape(bf16[1024,1280]{1,0:T(8,128)(2,1)} %gather_fusion.1) | data formatting | bytes 5242880 | tf_op jit(solution)/shard_map/jit(_take)/gather | solution.py:48
  497.1 12.2 %multiply_reduce_fusion = bf16[512,1280]{1,0:T(8,128)(2,1)} fusion(bf16[512,2,1280]{2,1,0:T(2,128)(2,1)} %gather.23, pred[512,2]{1,0:T(8,128)(4,1)S(1)} %copy.48, f32[512,2]{1,0:T(8,128)S(1)} %copy.42), kind=kLoop, calls=%fused_computation.8 | loop fusion | flops 4587520 | bytes 3937280 | tf_op jit(solution)/shard_map/reduce_sum | solution.py:50
  (65 shorter events, 13.0 us)
Async XLA Ops:
  0.0 27.8 %copy-start = (bf16[512,1280]{1,0:T(8,128)(2,1)S(1)}, bf16[512,1280]{1,0:T(8,128)(2,1)}, u32[]{:S(2)}) copy-start(bf16[512,1280]{1,0:T(8,128)(2,1)} %param.8) | copy-start | bytes 3932164
  11.5 26.1 %copy-start.3 = (s32[1024]{0:T(1024)}, s32[1024]{0:T(1024)S(1)}, u32[]{:S(2)}) copy-start(s32[1024]{0:T(1024)S(1)} %broadcast_add_fusion.1) | copy-start | bytes 12292
  11.9 11.4 %copy-start.5 = (s32[1024,1]{0,1:T(1,128)}, s32[1024,1]{0,1:T(1,128)S(1)}, u32[]{:S(2)}) copy-start(s32[1024,1]{0,1:T(1,128)S(1)} %compare_select_fusion) | copy-start | bytes 12292
  16.9 26.1 %all-to-all-start.1 = ((s32[32,1,64]{2,1,0:T(1,128)}), s32[32,1,64]{2,1,0:T(1,128)S(1)}, u32[]{:S(2)}, u32[]{:S(2)}) async-start(s32[32,1,64]{2,1,0:T(1,128)} %all_to_all.13), calls=%async_computation.1 | async-start | bytes 32768 | tf_op jit(solution)/shard_map/all_to_all | solution.py:40
  43.0 122.2 %all-to-all-start = ((bf16[32,64,1280]{2,1,0:T(8,128)(2,1)}), bf16[32,64,1280]{2,1,0:T(8,128)(2,1)}, u32[]{:S(2)}, u32[]{:S(2)}) async-start(bf16[32,64,1280]{2,1,0:T(8,128)(2,1)} %broadcast_select_fusion.2), calls=%async_computation | async-start | bytes 10485760 | tf_op jit(solution)/shard_map/all_to_all | solution.py:39
  306.9 57.7 %copy-start.4 = (s32[1024]{0:T(1024)S(1)}, s32[1024]{0:T(1024)}, u32[]{:S(2)}) copy-start(s32[1024]{0:T(1024)} %copy-done.3) | copy-start | bytes 12292
  306.9 57.9 %copy-start.2 = (s32[512,2]{0,1:T(2,128)S(1)}, s32[512,2]{0,1:T(2,128)}, u32[]{:S(2)}) copy-start(s32[512,2]{0,1:T(2,128)} %param.10) | copy-start | bytes 12292
  306.9 58.3 %copy-start.1 = (f32[1280,32]{0,1:T(8,128)S(1)}, f32[1280,32]{0,1:T(8,128)}, u32[]{:S(2)}) copy-start(f32[1280,32]{0,1:T(8,128)} %param.9) | copy-start | bytes 491524
  306.9 174.0 %all-to-all-start.2 = ((bf16[32,64,1280]{2,1,0:T(8,128)(2,1)}), bf16[32,64,1280]{2,1,0:T(8,128)(2,1)}, u32[]{:S(2)}, u32[]{:S(2)}) async-start(bf16[32,64,1280]{2,1,0:T(8,128)(2,1)} %bitcast.29), calls=%async_computation.2 | async-start | bytes 10485760 | tf_op jit(solution)/shard_map/all_to_all | solution.py:47
  365.8 9.5 %copy-start.6 = (s32[1024,1]{0,1:T(1,128)S(1)}, s32[1024,1]{0,1:T(1,128)}, u32[]{:S(2)}) copy-start(s32[1024,1]{0,1:T(1,128)} %copy-done.5) | copy-start | bytes 12292
where the time goes:
time: 510 us; the launch traced here: 509 us
  waiting for transfers between devices  209 us (41%)
  other arithmetic  90.9 us (18%)
  local copies, waits for them, and re-layouts  78.3 us (15%)
  starting transfers between devices  70 us (14%)
  Pallas kernels  60.7 us (12%)
    all_to_all x1, waiting for transfers between devices, device_body(): lax.all_to_all(out_rows.reshape(dev_count, row_cap, model_dim), 'ep', 0,...  106 us
    all_to_all x1, waiting for transfers between devices, device_body(): recv_rows = lax.all_to_all(send_rows, 'ep', 0, 0, tiled=True)  103 us
    another operation x3, Pallas kernels  59.5 us
    all_to_all x1, starting transfers between devices, device_body(): lax.all_to_all(out_rows.reshape(dev_count, row_cap, model_dim), 'ep', 0,...  57.7 us
    convert_element_type x1, other arithmetic, expert_ffn(): act_rows = (jax.nn.silu(h_one) * h_three).astype(jnp.bfloat16)  34.1 us
    gather x2, local copies, waits for them, and re-layouts, device_body(): jnp.take(back_rows.reshape(dev_count * row_cap, model_dim), slot_pos, axi...  16.2 us
    gather x1, local copies, waits for them, and re-layouts, device_body(): out_rows = jnp.take(out_sorted, jnp.argsort(sort_order), axis=0)  15.2 us
    gather x1, local copies, waits for them, and re-layouts, device_body(): jnp.take(recv_rows.reshape(dev_count * row_cap, model_dim), sort_order, a...  15.2 us
  transfers between devices with their start and end apart: 3, of which 2 were waited for; matrix products, arithmetic and copies ran while one was open for 8% of the time, Pallas kernels for 0%

commit v1 on v0

v1 whole, which is shorter than its diff:
```python
import functools

import jax
import jax.numpy as jnp
from jax import lax
from jax.experimental import pallas as pl
from jax.experimental.pallas import tpu as pltpu
from jax.sharding import PartitionSpec as P

MESH = pl.DeviceIdType.MESH
PLANES = 4
SIDE = 8
BUCKET = 64
TILE = 512


def xor_bits(a, b, bits):
    total = 0
    for bit in range(bits):
        step = 1 << bit
        total = total + ((a // step + b // step) % 2) * step
    return total


def moe_kernel(cap, x, pos_row, pos_col, gates, meta, w1, w3, w2, out, ysend, zbuf, metain, bsend, xin, ein, rsend, rin, acc, outacc, wb1, wb3, wb2, wsem, ysem, zsem, msem, mrsem, bsem, xsem, esem, eisem, rsem, rinsem):
    tok, model = x.shape
    rows = SIDE * BUCKET
    n_tiles = w1.shape[2] // TILE
    n_steps = PLANES * n_tiles
    me = lax.axis_index("ep")
    plane, seat = me // SIDE, me % SIDE

    def column_peer(i):
        return xor_bits(plane, i, 2) * SIDE + seat

    def plane_peer(j):
        return plane * SIDE + xor_bits(seat, j, 3)

    def weight_copies(step):
        slot, cols = step % 2, pl.ds(pl.multiple_of((step % n_tiles) * TILE, TILE), TILE)
        return (
            pltpu.make_async_copy(w1.at[0, :, cols], wb1.at[slot], wsem.at[slot, 0]),
            pltpu.make_async_copy(w3.at[0, :, cols], wb3.at[slot], wsem.at[slot, 1]),
            pltpu.make_async_copy(w2.at[0, cols, :], wb2.at[slot], wsem.at[slot, 2]),
        )

    def remote(src, dst, send, recv, peer):
        return pltpu.make_async_remote_copy(src_ref=src, dst_ref=dst, send_sem=send, recv_sem=recv, device_id=(peer,), device_id_type=MESH)

    def y_copy(i):
        return remote(ysend.at[i - 1], zbuf.at[i], ysem.at[i], zsem.at[i], column_peer(i))

    def meta_copy(i):
        return remote(meta.at[i], metain.at[i], msem.at[i], mrsem.at[i], column_peer(i))

    def bucket(j):
        return pl.ds(j * BUCKET, BUCKET)

    def b_copy(i, j):
        return remote(bsend.at[i, bucket(j)], xin.at[i, bucket(j)], bsem.at[i, j], xsem.at[i, j], plane_peer(j))

    def e_copy(i, j):
        return remote(bsend.at[i, bucket(j)], ein.at[i, bucket(j)], esem.at[i, j], eisem.at[i, j], plane_peer(j))

    def r_copy(i):
        return remote(rsend.at[i], rin.at[i], rsem.at[i], rinsem.at[i], column_peer(i))

    for copy in weight_copies(0):
        copy.start()

    barrier = pltpu.get_barrier_semaphore()
    for i in range(1, PLANES):
        pl.semaphore_signal(barrier, inc=1, device_id=(column_peer(i),), device_id_type=MESH)
    for j in range(1, SIDE):
        pl.semaphore_signal(barrier, inc=1, device_id=(plane_peer(j),), device_id_type=MESH)
    pl.semaphore_wait(barrier, PLANES - 1 + SIDE - 1)

    for i in range(1, PLANES):
        meta_copy(i).start()
    metain[0] = meta[0]

    def compact(i):
        want = lax.broadcasted_iota(jnp.int32, (cap, tok), 0)
        hit = (want == pos_row[2 * i : 2 * i + 1, :]) | (want == pos_row[2 * i + 1 : 2 * i + 2, :])
        return jnp.dot(hit.astype(jnp.float32).astype(jnp.bfloat16), x[...], preferred_element_type=jnp.float32).astype(jnp.bfloat16)

    ysend[0] = compact(1)
    ysend[1] = compact(2)
    y_copy(1).start()
    ysend[2] = compact(3)
    y_copy(2).start()
    zbuf[0] = compact(0)
    y_copy(3).start()

    def spread(i):
        diff = lax.broadcasted_iota(jnp.int32, (BUCKET, cap), 1) - lax.broadcasted_iota(jnp.int32, (BUCKET, cap), 0)
        hits = [(diff == metain[i, j : j + 1, :cap]).astype(jnp.float32).astype(jnp.bfloat16) for j in range(SIDE)]
        spread_rows = jnp.dot(jnp.concatenate(hits, axis=0), zbuf[i], preferred_element_type=jnp.float32).astype(jnp.bfloat16)
        bsend[i] = spread_rows
        for j in range(1, SIDE):
            b_copy(i, j).start()

    def collect(i):
        ein[i, 0:BUCKET] = bsend[i, 0:BUCKET]
        for j in range(1, SIDE):
            e_copy(i, j).wait_recv()
        hit = lax.broadcasted_iota(jnp.int32, (cap, rows), 0) == metain[i, SIDE : SIDE + 1, :]
        return jnp.dot(hit.astype(jnp.float32).astype(jnp.bfloat16), ein[i], preferred_element_type=jnp.float32).astype(jnp.bfloat16)

    spread(0)

    def tile_body(i, f, carry):
        step = i * n_tiles + f
        slot = step % 2

        @pl.when(step + 1 < n_steps)
        def _():
            for copy in weight_copies(step + 1):
                copy.start()

        for copy in weight_copies(step):
            copy.wait()
        up = jnp.dot(xin[i], wb1[slot], preferred_element_type=jnp.float32)
        gate = jnp.dot(xin[i], wb3[slot], preferred_element_type=jnp.float32)
        act = (jax.nn.silu(up) * gate).astype(jnp.bfloat16)
        acc[...] += jnp.dot(act, wb2[slot], preferred_element_type=jnp.float32)

        @pl.when((f == 3) & (i + 1 < PLANES))
        def _():
            y_copy(i + 1).wait_recv()
            meta_copy(i + 1).wait_recv()
            spread(i + 1)

        @pl.when((f == 7) & (i == 1))
        def _():
            rin[0] = collect(0)

        @pl.when((f == 7) & (i > 1))
        def _():
            rsend[i - 1] = collect(i - 1)
            r_copy(i - 1).start()

        return carry

    def block_body(i, carry):
        xin[i, 0:BUCKET] = bsend[i, 0:BUCKET]
        for j in range(1, SIDE):
            b_copy(i, j).wait_recv()
        acc[...] = jnp.zeros_like(acc)
        lax.fori_loop(0, n_tiles, functools.partial(tile_body, i), 0)
        for j in range(1, SIDE):
            b_copy(i, j).wait_send()
        bsend[i] = acc[...].astype(jnp.bfloat16)
        for j in range(1, SIDE):
            e_copy(i, j).start()
        return carry

    lax.fori_loop(0, PLANES, block_body, 0)
    rsend[PLANES - 1] = collect(PLANES - 1)
    r_copy(PLANES - 1).start()

    for i in range(PLANES):
        if i > 0:
            r_copy(i).wait_recv()
        seen = lax.broadcasted_iota(jnp.int32, (tok, cap), 1)
        first = (seen == pos_col[:, 2 * i : 2 * i + 1]).astype(jnp.float32).astype(jnp.bfloat16)
        second = (seen == pos_col[:, 2 * i + 1 : 2 * i + 2]).astype(jnp.float32).astype(jnp.bfloat16)
        mixed = gates[:, 0:1] * jnp.dot(first, rin[i], preferred_element_type=jnp.float32)
        mixed += gates[:, 1:2] * jnp.dot(second, rin[i], preferred_element_type=jnp.float32)
        if i == 0:
            outacc[...] = mixed
        elif i < PLANES - 1:
            outacc[...] += mixed
        else:
            out[...] = (outacc[...] + mixed).astype(jnp.bfloat16)

    for i in range(1, PLANES):
        y_copy(i).wait_send()
        meta_copy(i).wait_send()
        r_copy(i).wait_send()
    for i in range(PLANES):
        for j in range(1, SIDE):
            e_copy(i, j).wait_send()


def fused_moe(cap, x, pos_row, pos_col, gates, meta, w1, w3, w2):
    tok, model = x.shape
    rows = SIDE * BUCKET
    bf = jnp.bfloat16
    vmem = pl.BlockSpec(memory_space=pltpu.VMEM)
    hbm = pl.BlockSpec(memory_space=pl.ANY)
    dma = pltpu.SemaphoreType.DMA
    width = w1.shape[2]
    return pl.pallas_call(
        functools.partial(moe_kernel, cap),
        out_shape=jax.ShapeDtypeStruct((tok, model), bf),
        in_specs=[vmem] * 5 + [hbm] * 3,
        out_specs=vmem,
        scratch_shapes=[
            pltpu.VMEM((PLANES - 1, cap, model), bf),
            pltpu.VMEM((PLANES, cap, model), bf),
            pltpu.VMEM((PLANES, 2 * SIDE, rows), jnp.int32),
            pltpu.VMEM((PLANES, rows, model), bf),
            pltpu.VMEM((PLANES, rows, model), bf),
            pltpu.VMEM((PLANES, rows, model), bf),
            pltpu.VMEM((PLANES, cap, model), bf),
            pltpu.VMEM((PLANES, cap, model), bf),
            pltpu.VMEM((rows, model), jnp.float32),
            pltpu.VMEM((tok, model), jnp.float32),
            pltpu.VMEM((2, model, TILE), bf),
            pltpu.VMEM((2, model, TILE), bf),
            pltpu.VMEM((2, TILE, model), bf),
            dma((2, 3)),
            dma((PLANES,)),
            dma((PLANES,)),
            dma((PLANES,)),
            dma((PLANES,)),
            dma((PLANES, SIDE)),
            dma((PLANES, SIDE)),
            dma((PLANES, SIDE)),
            dma((PLANES, SIDE)),
            dma((PLANES,)),
            dma((PLANES,)),
        ],
        compiler_params=pltpu.CompilerParams(collective_id=0, has_side_effects=True, vmem_limit_bytes=67_000_000),
        cost_estimate=pl.CostEstimate(flops=6 * PLANES * rows * model * width, bytes_accessed=3 * PLANES * model * width * 2, transcendentals=0),
    )(x, pos_row, pos_col, gates, meta, w1, w3, w2)


def route(hidden, w_router, ids, me):
    experts = w_router.shape[1]
    tok = ids.shape[0]
    plane, seat = me // SIDE, me % SIDE
    logits = jnp.dot(hidden.astype(jnp.float32), w_router, preferred_element_type=jnp.float32)
    probs = jax.nn.softmax(logits, axis=-1)
    chosen = ids[:, :, None] == jnp.arange(experts)[None, None, :]
    picked = jnp.sum(jnp.where(chosen, probs[:, None, :], 0.0), axis=2)
    gates = picked / jnp.sum(picked, axis=1, keepdims=True)
    named = jnp.any(chosen, axis=1)
    before = (jnp.arange(tok)[:, None] > jnp.arange(tok)[None, :]).astype(jnp.bfloat16)
    rank = (jnp.dot(before, named.astype(jnp.bfloat16), preferred_element_type=jnp.float32) + 0.5).astype(jnp.int32)
    counts = jnp.sum(named.astype(jnp.int32), axis=0)
    lane = jnp.arange(experts)
    start = jnp.sum(jnp.where(lane[None, :] < lane[:, None], counts[None, :], 0), axis=1)
    pos = jnp.sum(jnp.where(chosen, (rank + start[None, :])[:, None, :], 0), axis=2)
    planes = plane ^ jnp.arange(PLANES)
    plane_start = jnp.sum(jnp.where(lane[None, :] == planes[:, None] * SIDE, start[None, :], 0), axis=1)
    mine = (ids // SIDE)[:, None, :] == planes[None, :, None]
    pos_col = jnp.where(mine, pos[:, None, :] - plane_start[None, :, None], -1).reshape(tok, 2 * PLANES)
    dest = planes[:, None] * SIDE + (seat ^ jnp.arange(SIDE))[None, :]
    at_dest = dest[:, :, None] == lane[None, None, :]
    dest_start = jnp.sum(jnp.where(at_dest, start[None, None, :], 0), axis=2) - plane_start[:, None]
    dest_count = jnp.sum(jnp.where(at_dest, counts[None, None, :], 0), axis=2)
    slot = jnp.arange(BUCKET)
    home = jnp.where(slot[None, None, :] < dest_count[:, :, None], dest_start[:, :, None] + slot[None, None, :], -1)
    wide = SIDE * BUCKET
    meta = jnp.concatenate(
        [
            jnp.broadcast_to(dest_start[:, :, None], (PLANES, SIDE, wide)),
            jnp.broadcast_to(home.reshape(PLANES, 1, wide), (PLANES, SIDE, wide)),
        ],
        axis=1,
    )
    most = jnp.max(jnp.sum(counts.reshape(PLANES, SIDE), axis=1))
    return gates, pos_col.T, pos_col, meta, most


CAPS = (512,)


def solution(mesh):
    def device_body(hidden_loc, w_router, ids_loc, w_one, w_three, w_two):
        me = lax.axis_index("ep")
        gates, pos_row, pos_col, meta, most = route(hidden_loc, w_router, ids_loc, me)
        if len(CAPS) == 1:
            return fused_moe(CAPS[0], hidden_loc, pos_row, pos_col, gates, meta, w_one, w_three, w_two)
        most = lax.pmax(most, "ep")
        pick = sum((most > cap).astype(jnp.int32) for cap in CAPS[:-1])
        branches = [functools.partial(fused_moe, cap) for cap in CAPS]
        return lax.switch(pick, branches, hidden_loc, pos_row, pos_col, gates, meta, w_one, w_three, w_two)

    return jax.shard_map(device_body, mesh=mesh, in_specs=(P("ep", None), P(None, None), P("ep", None), P("ep", None, None), P("ep", None, None), P("ep", None, None)), out_specs=P("ep", None), check_vma=False)
```

time: 510 us -> 290 us (0.57)
  the two profiles are of different devices: /device:TPU:5 before, /device:TPU:11 now
where the time goes in v1:
time: 290 us; the launch traced here: 289 us
  Pallas kernels  277 us (96%)
  local copies, waits for them, and re-layouts  5.07 us (2%)
  other arithmetic  4.65 us (2%)
    pallas_call x1, Pallas kernels, fused_moe(): pl.pallas_call(functools.partial(moe_kernel, cap), out_shape=jax.ShapeDty...  277 us

profile of v1, /device:TPU:11, one launch (start us, length us, event | category | flops | bytes accessed | tf_op | source)
XLA Modules:
  0.0 289.3 jit_solution(18193502978879009221)
XLA Ops:
  0.1 0.1 eq.64
  0.2 0.7 and_select_fusion
  1.0 0.1 lt.53
  1.1 0.7 fusion.2
  1.8 0.1 convert_reduce_fusion
  1.9 0.1 select_reduce_fusion.5
  2.0 0.2 select_reduce_fusion.6
  2.2 0.3 select_reduce_fusion.3
  2.5 0.1 broadcast_subtract_fusion
  2.6 0.1 sub.55
  2.8 0.1 lt.56
  2.9 0.1 add.63
  3.0 0.3 fusion.1
  3.3 0.7 select_reduce_fusion.2
  4.2 0.7 pad_add_fusion.meta
  4.8 1.8 fusion.5
  6.8 0.1 copy.23
  6.9 0.1 copy.22
  7.1 0.7 copy-done
  7.8 0.7 copy.26.pos_row
  8.5 0.1 copy.24
  8.6 0.9 broadcast_divide_fusion.gates
  9.5 277.4 %shard_map.64 = bf16[512,1280]{1,0:T(8,128)(2,1)} custom-call(bf16[512,1280]{1,0:T(8,128)(2,1)} %x.1, s32[8,512]{1,0:T(8,128)} %copy.26.pos_row, s32[512,8]{1,0:T(8,128)} %copy-done, f32[512,2]{1,0:T(8,128)} %broadcast_divide_fusion.gates, s32[4,16,512]{2,1,0:T(8,128)} %pad_add_fusion.meta, bf16[1,1280,5120]{2,1,0:T(8,128)(2,1)} %w1.1, ...), custom_call_target="tpu_custom_call" | custom-call | flops 80530636800 | bytes 157286400 | tf_op jit(solution)/shard_map/pallas_call | solution.py:194
  286.9 2.5 copy.28
  (24 shorter events, 0.6 us)
Async XLA Ops:
  0.0 4.8 %copy-start.1 = (f32[1280,32]{0,1:T(8,128)S(1)}, f32[1280,32]{0,1:T(8,128)}, u32[]{:S(2)}) copy-start(f32[1280,32]{0,1:T(8,128)} %param.7) | copy-start | bytes 491524
  3.0 3.7 %copy-start.2 = (s32[512,2]{0,1:T(2,128)S(1)}, s32[512,2]{0,1:T(2,128)}, u32[]{:S(2)}) copy-start(s32[512,2]{0,1:T(2,128)} %param.8) | copy-start | bytes 12292
  7.1 0.7 copy-start
